TPU v7x, 32 devices: a whole 2x2x4 slice. The times are simulated.
32 devices in a mesh: dp: 4 (over z), tensor: 8 (over y, x, core).
Axes of the slice: x: 2, y: 2, z: 4, core: 2. Of those that a mesh axis runs over, the one named last changes fastest.
Arguments:
- tokens: bfloat16 [1024, 4096], P(('dp', 'tensor')), may hold values from -4 to 4
- lengths: int32 [4], replicated, may hold values from 64 to 256, as said below
- norm_gains: float32 [2, 4096], replicated, may hold values from 0.25 to 1.75
- query_weight: bfloat16 [2, 4096, 4096], P(None, None, 'tensor'), may hold values from -0.09375 to 0.09375
- key_weight: bfloat16 [2, 4096, 1024], P(None, None, 'tensor'), may hold values from -0.09375 to 0.09375
- value_weight: bfloat16 [2, 4096, 1024], P(None, None, 'tensor'), may hold values from -0.09375 to 0.09375
- out_weight: bfloat16 [2, 4096, 4096], P(None, 'tensor'), may hold values from -0.09375 to 0.09375
- query_probe: bfloat16 [2, 4096, 4096], P(None, 'dp', 'tensor'), may hold values from -0.09375 to 0.09375
- key_probe: bfloat16 [2, 4096, 1024], P(None, 'dp', 'tensor'), may hold values from -0.09375 to 0.09375
- value_probe: bfloat16 [2, 4096, 1024], P(None, 'dp', 'tensor'), may hold values from -0.09375 to 0.09375
- out_probe: bfloat16 [2, 4096, 4096], P(None, 'tensor', 'dp'), may hold values from -0.09375 to 0.09375
Outputs:
- query_product: float32 [2, 4096, 4096], P(None, 'dp', 'tensor')
- key_product: float32 [2, 4096, 1024], P(None, 'dp', 'tensor')
- value_product: float32 [2, 4096, 1024], P(None, 'dp', 'tensor')
- out_product: float32 [2, 4096, 4096], P(None, 'tensor', 'dp')
Inputs may be any that keep to these rules, and one draw needn't show every extreme that they name: lengths[i] counts the leading valid positions of sequence i; the last sequence is full.
All inputs are finite; a program needn't handle non-finite values.
Results may differ from a plain program's by a relative error of at most 0.035.
Values may be sent and summed in bfloat16 or wider, within the bound.
A program may use at most 128 MiB of HBM per device.

v0:
```python
import functools
import math

import jax
import jax.numpy as jnp
from jax import lax
from jax.experimental import pallas as pl
from jax.experimental.pallas import tpu as pltpu
from jax.sharding import PartitionSpec as P

HD = 128
LEN = 256
EPS = 1e-05
THETA = 500000.0
MESH = pl.DeviceIdType.MESH
SCALE = 1.0 / math.sqrt(HD)


def low(values):
    return values.astype(jnp.bfloat16)


def wide(values):
    return values.astype(jnp.float32)


def matmul(left_side, right_side):
    return jnp.dot(left_side, right_side, preferred_element_type=jnp.float32)


def contract_rows(left_side, right_side):
    return lax.dot_general(
        left_side, right_side, (((0,), (0,)), ((), ())), preferred_element_type=jnp.float32
    )


def contract_last(left_side, right_side):
    return lax.dot_general(
        left_side, right_side, (((1,), (1,)), ((), ())), preferred_element_type=jnp.float32
    )


def rope_tables(length, head_size):
    position = jnp.arange(length).astype(jnp.float32)
    column = jnp.arange(head_size // 2).astype(jnp.float32)
    frequency = jnp.exp(-math.log(THETA) * 2.0 * column / head_size)
    angles = position[:, None] * frequency[None, :]
    cosine, sine = jnp.cos(angles), jnp.sin(angles)
    return (
        jnp.concatenate([cosine, cosine], axis=-1),
        jnp.concatenate([-sine, sine], axis=-1),
    )


def flip(index, mask):
    result = index
    bit = 1
    while bit <= mask:
        if mask & bit:
            result = result + bit - 2 * bit * lax.rem(lax.div(index, bit), 2)
        bit *= 2
    return result


def semaphore_count(sizes):
    batches, width = sizes
    return 4 * width + 3 * batches


class Fabric:
    def __init__(self, sizes, send, recv):
        self.batches, self.width = sizes
        self.chips = self.width // 2
        self.row = lax.axis_index("dp")
        self.col = lax.axis_index("tensor")
        self.send, self.recv, self.used = send, recv, 0
        self.pending = []

    def copy(self, source, target, row, col):
        number = self.used
        self.used += 1
        assert number < semaphore_count((self.batches, self.width))
        made = pltpu.make_async_remote_copy(
            src_ref=source,
            dst_ref=target,
            send_sem=self.send.at[number],
            recv_sem=self.recv.at[number],
            device_id=(row, col),
            device_id_type=MESH,
        )
        made.start()
        self.pending.append(made)
        return made

    def drain(self):
        for made in self.pending:
            made.wait_send()

    def mate(self):
        return flip(self.col, 1)

    def peer(self, step):
        return flip(self.col, 2 * step)

    def batch(self, step):
        return flip(self.row, step)

    def greet(self, along_tensor=True):
        barrier = pltpu.get_barrier_semaphore()
        peers = [(self.batch(step), self.col) for step in range(1, self.batches)]
        if along_tensor:
            peers += [(self.row, self.peer(step)) for step in range(1, self.chips)]
            peers.append((self.row, self.mate()))
        for peer in peers:
            pl.semaphore_signal(barrier, inc=1, device_id=peer, device_id_type=MESH)
        return lambda: pl.semaphore_wait(barrier, len(peers))

    def gather(self, source, slot):
        there = slot(self.col)
        direct = [
            self.copy(source, there, self.row, self.peer(step)) for step in range(1, self.chips)
        ]
        beside = [self.copy(source, there, self.row, self.mate())]
        there[...] = source[...]

        def forward():
            for step in range(1, self.chips):
                direct[step - 1].wait_recv()
                piece = slot(self.peer(step))
                beside.append(self.copy(piece, piece, self.row, self.mate()))

        def finish():
            for made in beside:
                made.wait_recv()

        return forward, finish

    def pair_up(self, slot, beside):
        return [
            self.copy(slot(flip(self.mate(), 2 * step)), beside.at[step], self.row, self.mate())
            for step in range(self.chips)
        ]

    def spread(self, slot, copies, beside, summed, landed):
        sent = []
        order = list(range(self.chips - 1, 0, -1))
        for place, step in enumerate(order):
            copies[step].wait_recv()
            summed[step] = low(wide(slot(self.peer(step))[...]) + wide(beside[step]))
            if place:
                last = order[place - 1]
                sent.append(
                    self.copy(summed.at[last], landed.at[last], self.row, self.peer(last))
                )
        copies[0].wait_recv()
        total = wide(slot(self.col)[...]) + wide(beside[0])
        if order:
            last = order[-1]
            sent.append(self.copy(summed.at[last], landed.at[last], self.row, self.peer(last)))

        def finish():
            result = total
            for made, step in zip(sent, order):
                made.wait_recv()
                result = result + wide(landed[step])
            return result

        return finish

    def exchange(self, source, target):
        made = [
            self.copy(
                source.at[self.batch(step)], target.at[self.row], self.batch(step), self.col
            )
            for step in range(1, self.batches)
        ]
        target[self.row] = source[self.row]

        def finish():
            for copy in made:
                copy.wait_recv()

        return finish

    def scatter_batch(self, source, landed, steps):
        return [
            self.copy(
                source.at[self.batch(step)], landed.at[step], self.batch(step), self.col
            )
            for step in steps
        ]

    def gather_batch(self, source, target):
        made = [
            self.copy(source, target.at[self.row], self.batch(step), self.col)
            for step in range(1, self.batches)
        ]
        target[self.row] = source[...]
        return made


def inverse_of(stream):
    return lax.rsqrt(jnp.mean(stream * stream, axis=-1, keepdims=True) + EPS)


def set_shard(values, shard, pieces):
    rounded = low(values)
    shard[...] = rounded
    block = pieces.shape[-1]
    for number in range(pieces.shape[0]):
        pieces[number] = rounded[:, number * block : (number + 1) * block]


def gather_both(fabric, shard, pieces, exchanged, whole, blocks):
    arrived = fabric.exchange(pieces, exchanged)
    forward, finish = fabric.gather(shard, lambda col: whole.at[col])
    arrived()
    forward_blocks, finish_blocks = fabric.gather(exchanged, lambda col: blocks.at[:, col])
    forward()
    forward_blocks()
    finish()
    finish_blocks()


def add_landed(own, landed, copies, steps):
    total = wide(own)
    for made, step in zip(copies, steps):
        made.wait_recv()
        total = total + wide(landed[step])
    return total


def open_kernel(sizes, tokens, gain, whole, blocks, shard, pieces, exchanged, send, recv):
    fabric = Fabric(sizes, send, recv)
    ready = fabric.greet()
    stream = wide(tokens[...])
    set_shard(stream * inverse_of(stream) * gain[...], shard, pieces)
    ready()
    gather_both(fabric, shard, pieces, exchanged, whole, blocks)
    fabric.drain()


def second_kernel(
    sizes,
    terms,
    tokens,
    gain,
    partial,
    blended,
    stream_out,
    whole,
    blocks,
    moved,
    blended_all,
    beside,
    summed,
    landed,
    shard,
    pieces,
    exchanged,
    returned,
    send,
    recv,
):
    fabric = Fabric(sizes, send, recv)
    fabric.greet()()
    slot = lambda col: terms.at[col]
    paired = fabric.pair_up(slot, beside)
    steps = list(range(1, fabric.batches))
    back = fabric.scatter_batch(partial, returned, steps)
    total = fabric.spread(slot, paired, beside, summed, landed)()
    rounded = low(wide(tokens[...]) + total)
    stream_out[...] = rounded
    stream = wide(rounded)
    set_shard(stream * inverse_of(stream) * gain[...], shard, pieces)
    gather_both(fabric, shard, pieces, exchanged, whole, blocks)
    fetched = fabric.gather_batch(blended, blended_all)
    moved[...] = add_landed(partial[fabric.row], returned, back, steps)
    for made in fetched:
        made.wait_recv()
    fabric.drain()


def tangent_total(fabric, terms, probed, beside, summed, landed, probe_bufs, pieces, exchanged):
    beside_p, summed_p, landed_p = probe_bufs
    slot = lambda col: terms.at[col]
    slot_p = lambda col: probed.at[:, col]
    paired_p = fabric.pair_up(slot_p, beside_p)
    paired = fabric.pair_up(slot, beside)
    finish_p = fabric.spread(slot_p, paired_p, beside_p, summed_p, landed_p)
    finish = fabric.spread(slot, paired, beside, summed, landed)
    pieces[...] = low(finish_p())
    total = finish()
    fabric.exchange(pieces, exchanged)()
    block = pieces.shape[-1]
    return [
        total[:, number * block : (number + 1) * block] + wide(exchanged[number])
        for number in range(fabric.batches)
    ]


def third_kernel(
    sizes,
    terms,
    probed,
    stream_in,
    gain,
    partial,
    blended,
    tangent,
    whole,
    moved,
    blended_all,
    beside,
    summed,
    landed,
    beside_p,
    summed_p,
    landed_p,
    shard,
    pieces,
    exchanged,
    returned,
    send,
    recv,
):
    fabric = Fabric(sizes, send, recv)
    fabric.greet()()
    steps = list(range(1, fabric.batches))
    early = steps[: (len(steps) + 1) // 2]
    back = fabric.scatter_batch(partial, returned, early)
    parts = tangent_total(
        fabric, terms, probed, beside, summed, landed, (beside_p, summed_p, landed_p),
        pieces, exchanged,
    )
    back += fabric.scatter_batch(partial, returned, steps[len(early) :])
    change = jnp.concatenate(parts, axis=-1)
    tangent[...] = change
    stream = wide(stream_in[...])
    inverse = inverse_of(stream)
    shift = jnp.mean(stream * change, axis=-1, keepdims=True)
    shard[...] = low(
        gain[...] * (change * inverse - stream * inverse * inverse * inverse * shift)
    )
    fetched = fabric.gather_batch(blended, blended_all)
    forward, finish = fabric.gather(shard, lambda col: whole.at[col])
    forward()
    finish()
    moved[...] = add_landed(partial[fabric.row], returned, back, steps)
    for made in fetched:
        made.wait_recv()
    fabric.drain()


def fourth_kernel(
    sizes,
    terms,
    probed,
    tangent,
    mask,
    cotangent,
    whole,
    blocks,
    beside,
    summed,
    landed,
    beside_p,
    summed_p,
    landed_p,
    shard,
    pieces,
    exchanged,
    pieces_p,
    exchanged_p,
    send,
    recv,
):
    fabric = Fabric(sizes, send, recv)
    fabric.greet()()
    parts = tangent_total(
        fabric, terms, probed, beside, summed, landed, (beside_p, summed_p, landed_p),
        pieces_p, exchanged_p,
    )
    change = jnp.concatenate(parts, axis=-1)
    result = mask[...] * (tangent[...] + change)
    cotangent[...] = result
    set_shard(result, shard, pieces)
    gather_both(fabric, shard, pieces, exchanged, whole, blocks)
    fabric.drain()


def fifth_kernel(
    sizes,
    terms,
    stream_in,
    gain,
    cotangent,
    grads,
    cotangent_out,
    whole,
    blocks,
    grads_all,
    beside,
    summed,
    landed,
    shard,
    pieces,
    exchanged,
    send,
    recv,
):
    fabric = Fabric(sizes, send, recv)
    fabric.greet()()
    slot = lambda col: terms.at[col]
    paired = fabric.pair_up(slot, beside)
    total = fabric.spread(slot, paired, beside, summed, landed)()
    stream = wide(stream_in[...])
    inverse = inverse_of(stream)
    scaled = total * gain[...]
    shift = jnp.mean(stream * scaled, axis=-1, keepdims=True)
    result = cotangent[...] + inverse * (scaled - stream * inverse * inverse * shift)
    cotangent_out[...] = result
    set_shard(result, shard, pieces)
    gather_both(fabric, shard, pieces, exchanged, whole, blocks)
    fetched = fabric.gather_batch(grads, grads_all)
    for made in fetched:
        made.wait_recv()
    fabric.drain()


def last_kernel(sizes, grads, grads_all, send, recv):
    fabric = Fabric(sizes, send, recv)
    fabric.greet(along_tensor=False)()
    for made in fabric.gather_batch(grads, grads_all):
        made.wait_recv()
    fabric.drain()


def communicate(kernel, sizes, number, inputs, outputs, scratch):
    vmem = pl.BlockSpec(memory_space=pltpu.VMEM)
    return pl.pallas_call(
        functools.partial(kernel, sizes),
        out_shape=[jax.ShapeDtypeStruct(shape, kind) for shape, kind in outputs],
        in_specs=[vmem] * len(inputs),
        out_specs=[vmem] * len(outputs),
        scratch_shapes=[pltpu.VMEM(shape, jnp.bfloat16) for shape in scratch]
        + [pltpu.SemaphoreType.DMA((semaphore_count(sizes),))] * 2,
        compiler_params=pltpu.CompilerParams(collective_id=number, has_side_effects=True),
    )(*inputs)


def turn(values, cosine, sine, direction):
    other = pltpu.roll(values, HD // 2, 1)
    if direction > 0:
        return values * cosine + other * sine
    return values * cosine - other * sine


def head(index):
    return slice(index * HD, (index + 1) * HD)


def allowed_keys(length):
    row_index = lax.broadcasted_iota(jnp.int32, (LEN, LEN), 0)
    column_index = lax.broadcasted_iota(jnp.int32, (LEN, LEN), 1)
    return (column_index <= row_index) & (column_index < length)


def softmax_weights(queries, keys, allowed):
    powers = jnp.where(allowed, jnp.exp(contract_last(queries, keys) * SCALE), 0.0)
    return powers / jnp.sum(powers, axis=-1, keepdims=True)


def centred(weights, values):
    return weights * (values - jnp.sum(weights * values, axis=-1, keepdims=True))


def each_head(total_rows, query_width, key_width):
    repeat = query_width // key_width
    for seq in range(total_rows // LEN):
        rows = slice(seq * LEN, (seq + 1) * LEN)
        for number in range(key_width // HD):
            yield seq, rows, number, range(number * repeat, (number + 1) * repeat)


def primal_kernel(
    steps,
    with_out,
    lengths,
    normed,
    query_weight,
    key_weight,
    value_weight,
    blocks,
    query_probe,
    key_probe,
    value_probe,
    cosine,
    sine,
    *rest,
):
    if with_out:
        out_weight, queries, keys, values, blended, partial, out, acc_q, acc_k, acc_v = rest
    else:
        queries, keys, values, blended, partial, acc_q, acc_k, acc_v = rest
    step = pl.program_id(0)

    @pl.when(step == 0)
    def _():
        acc_q[...] = jnp.zeros_like(acc_q)
        acc_k[...] = jnp.zeros_like(acc_k)
        acc_v[...] = jnp.zeros_like(acc_v)

    @pl.when(step < steps)
    def _():
        part = normed[...]
        acc_q[...] += matmul(part, query_weight[0])
        acc_k[...] += matmul(part, key_weight[0])
        acc_v[...] += matmul(part, value_weight[0])
        rows = blocks[...]
        query_width = query_probe.shape[-1]
        partial[:, :query_width] = low(matmul(rows, query_probe[0]))
        partial[:, query_width:] = low(
            jnp.concatenate([matmul(rows, key_probe[0]), matmul(rows, value_probe[0])], axis=-1)
        )

    @pl.when(step == steps - 1)
    def _():
        values[...] = low(acc_v[...])
        total_rows, query_width = queries.shape
        for seq, rows, number, members in each_head(total_rows, query_width, keys.shape[1]):
            allowed = allowed_keys(lengths[seq])
            key_head = low(turn(acc_k[rows, head(number)], cosine[...], sine[...], 1))
            keys[rows, head(number)] = key_head
            value_head = low(acc_v[rows, head(number)])
            for member in members:
                query_head = low(turn(acc_q[rows, head(member)], cosine[...], sine[...], 1))
                queries[rows, head(member)] = query_head
                weights = low(softmax_weights(query_head, key_head, allowed))
                blended[rows, head(member)] = low(matmul(weights, value_head))

    if with_out:

        @pl.when(step >= steps)
        def _():
            out[...] = low(matmul(blended[...], out_weight[0]))


def tangent_kernel(
    steps,
    with_tangent,
    lengths,
    queries,
    keys,
    values,
    moved,
    cosine,
    sine,
    out_weight,
    blended_all,
    out_probe,
    *rest,
):
    if with_tangent:
        tangent, query_weight, key_weight, value_weight, terms, probed, acc, mixed = rest
    else:
        terms, probed, acc, mixed = rest
    step = pl.program_id(0)
    query_width, key_width = queries.shape[1], keys.shape[1]

    @pl.when(step == 0)
    def _():
        acc[...] = moved[...]

    if with_tangent:

        @pl.when(step < steps)
        def _():
            part = tangent[...]
            acc[:, :query_width] += matmul(part, query_weight[0])
            acc[:, query_width : query_width + key_width] += matmul(part, key_weight[0])
            acc[:, query_width + key_width :] += matmul(part, value_weight[0])

    @pl.when(step == steps - 1)
    def _():
        for seq, rows, number, members in each_head(queries.shape[0], query_width, key_width):
            allowed = allowed_keys(lengths[seq])
            key_head = keys[rows, head(number)]
            value_head = values[rows, head(number)]
            key_at = query_width // HD + number
            value_at = key_at + key_width // HD
            moved_key = low(turn(acc[rows, head(key_at)], cosine[...], sine[...], 1))
            moved_value = low(acc[rows, head(value_at)])
            for member in members:
                query_head = queries[rows, head(member)]
                moved_query = low(turn(acc[rows, head(member)], cosine[...], sine[...], 1))
                weights = softmax_weights(query_head, key_head, allowed)
                scores = SCALE * (
                    contract_last(moved_query, key_head) + contract_last(query_head, moved_key)
                )
                moved_weights = low(centred(weights, scores))
                mixed[rows, head(member)] = low(
                    matmul(moved_weights, value_head) + matmul(low(weights), moved_value)
                )

    @pl.when(step >= steps)
    def _():
        terms[...] = low(matmul(mixed[...], out_weight[0]))
        probed[...] = low(matmul(blended_all[...], out_probe[0]))


def backward_kernel(
    steps,
    with_grad,
    lengths,
    cotangent,
    out_weight,
    queries,
    keys,
    values,
    cosine,
    sine,
    *rest,
):
    if with_grad:
        query_weight, key_weight, value_weight, grads, terms, acc = rest
    else:
        grads, acc = rest
    step = pl.program_id(0)
    query_width, key_width = queries.shape[1], keys.shape[1]

    @pl.when(step == 0)
    def _():
        acc[...] = jnp.zeros_like(acc)

    @pl.when(step < steps)
    def _():
        acc[...] += contract_last(cotangent[...], out_weight[0])

    @pl.when(step == steps - 1)
    def _():
        for seq, rows, number, members in each_head(queries.shape[0], query_width, key_width):
            allowed = allowed_keys(lengths[seq])
            key_head = keys[rows, head(number)]
            value_head = values[rows, head(number)]
            key_at = query_width // HD + number
            value_at = key_at + key_width // HD
            key_total = jnp.zeros((LEN, HD), jnp.float32)
            value_total = jnp.zeros((LEN, HD), jnp.float32)
            for member in members:
                query_head = queries[rows, head(member)]
                mixed = low(acc[rows, head(member)])
                weights = softmax_weights(query_head, key_head, allowed)
                value_total = value_total + contract_rows(low(weights), mixed)
                scores = low(centred(weights, contract_last(mixed, value_head)) * SCALE)
                grads[rows, head(member)] = low(
                    turn(matmul(scores, key_head), cosine[...], sine[...], -1)
                )
                key_total = key_total + contract_rows(scores, query_head)
            grads[rows, head(key_at)] = low(turn(key_total, cosine[...], sine[...], -1))
            grads[rows, head(value_at)] = low(value_total)

    if with_grad:

        @pl.when(step >= steps)
        def _():
            terms[...] = low(
                contract_last(grads[:, :query_width], query_weight[0])
                + contract_last(grads[:, query_width : query_width + key_width], key_weight[0])
                + contract_last(grads[:, query_width + key_width :], value_weight[0])
            )


def product_kernel(layers, *refs):
    inputs, (query_out, key_out, value_out, out_out) = refs[:-4], refs[-4:]
    layer = pl.program_id(0)
    query_width, key_width = query_out.shape[-1], key_out.shape[-1]
    for number in range(layers):
        blocks, grads, blended, cotangent = inputs[4 * number : 4 * number + 4]

        @pl.when(layer == number)
        def _():
            product = contract_rows(blocks[...], grads[...])
            query_out[0] = product[:, :query_width]
            key_out[0] = product[:, query_width : query_width + key_width]
            value_out[0] = product[:, query_width + key_width :]
            out_out[0] = contract_rows(blended[...], cotangent[...])


CUTS = 4
FULL = None


def body(
    tokens,
    lengths,
    norm_gains,
    query_weight,
    key_weight,
    value_weight,
    out_weight,
    query_probe,
    key_probe,
    value_probe,
    out_probe,
):
    width = lax.axis_size("tensor")
    batches = lax.axis_size("dp")
    sizes = (batches, width)
    tensor_index = lax.axis_index("tensor")
    data_index = lax.axis_index("dp")
    share, model = tokens.shape
    group = share * width
    seq_count = group // LEN
    layers = query_weight.shape[0]
    assert layers == 2
    half_width = key_weight.shape[2]
    query_width = query_weight.shape[2]
    paired = half_width < HD
    key_width = 2 * half_width if paired else half_width
    sent_width = query_width + 2 * half_width
    block = query_probe.shape[1]
    chips = width // 2
    bf, f32 = jnp.bfloat16, jnp.float32
    cosine, sine = rope_tables(LEN, HD)
    group_lengths = lax.dynamic_slice_in_dim(lengths, data_index * seq_count, seq_count)
    position = tensor_index * share + jnp.arange(share)
    row_mask = wide(position % LEN < group_lengths[position // LEN])[:, None]
    lower_half = tensor_index % 2 == 0

    def swapped(value):
        pairs = [(source, source ^ 1) for source in range(width)]
        return lax.ppermute(value, "tensor", pairs)

    def join_halves(own_part):
        other_part = swapped(own_part)
        return jnp.where(
            lower_half,
            jnp.concatenate([own_part, other_part], axis=-1),
            jnp.concatenate([other_part, own_part], axis=-1),
        )

    def split_halves(values):
        first, second = values[:, :half_width], values[:, half_width:]
        own_part = jnp.where(lower_half, first, second)
        other_part = jnp.where(lower_half, second, first)
        return low(wide(own_part) + wide(swapped(other_part)))

    if paired:
        key_full, value_full = join_halves(key_weight), join_halves(value_weight)
    else:
        key_full, value_full = key_weight, value_weight

    def join_moved(moved):
        if not paired:
            return moved
        return jnp.concatenate(
            [
                moved[:, :query_width],
                join_halves(moved[:, query_width : query_width + half_width]),
                join_halves(moved[:, query_width + half_width :]),
            ],
            axis=-1,
        )

    def to_send(grads):
        if not paired:
            return grads
        return jnp.concatenate(
            [
                grads[:, :query_width],
                split_halves(grads[:, query_width : query_width + key_width]),
                split_halves(grads[:, query_width + key_width :]),
            ],
            axis=-1,
        )

    whole_shape = ((width, share, model), bf)
    blocks_shape = ((batches, width, share, block), bf)
    shard_shape = (share, model)
    pieces_shape = (batches, share, block)
    sum_shape = (chips, share, model)
    probe_shape = (chips, batches, share, block)
    back_shape = (batches, group, sent_width)
    rows_in_all = batches * group
    gains = [norm_gains[number][None] for number in range(layers)]
    cut = model // CUTS
    rows_cut = rows_in_all // CUTS

    def spec(shape, index):
        return pl.BlockSpec(shape, index)

    def fixed(shape):
        return pl.BlockSpec(shape, lambda i: (0,) * len(shape))

    def first_part(i):
        return jnp.minimum(i, CUTS - 1)

    def late_part(start):
        return lambda i: jnp.maximum(i - start, 0)

    smem = pl.BlockSpec(memory_space=pltpu.SMEM)
    table = fixed((LEN, HD))
    arbitrary = pltpu.CompilerParams(dimension_semantics=("arbitrary",))

    def cost(flops, moved_bytes):
        return pl.CostEstimate(flops=flops, bytes_accessed=moved_bytes, transcendentals=0)

    def weight_specs(layer, place):
        return [
            spec((1, cut, query_width), lambda i: (layer, place(i), 0)),
            spec((1, cut, key_width), lambda i: (layer, place(i), 0)),
            spec((1, cut, key_width), lambda i: (layer, place(i), 0)),
        ]

    def primal(layer, normed_all, blocks):
        with_out = layer < layers - 1
        late = late_part(CUTS)
        in_specs = [
            smem,
            spec((group, cut), lambda i: (0, first_part(i))),
            *weight_specs(layer, first_part),
            spec((rows_cut, block), lambda i: (first_part(i), 0)),
            spec((1, block, query_width), lambda i: (layer, 0, 0)),
            spec((1, block, half_width), lambda i: (layer, 0, 0)),
            spec((1, block, half_width), lambda i: (layer, 0, 0)),
            table,
            table,
        ]
        out_shape = [
            ((group, query_width), bf),
            ((group, key_width), bf),
            ((group, key_width), bf),
            ((group, query_width), bf),
            ((rows_in_all, sent_width), bf),
        ]
        out_specs = [
            fixed((group, query_width)),
            fixed((group, key_width)),
            fixed((group, key_width)),
            fixed((group, query_width)),
            spec((rows_cut, sent_width), lambda i: (first_part(i), 0)),
        ]
        args = [
            group_lengths,
            normed_all,
            query_weight,
            key_full,
            value_full,
            blocks,
            query_probe,
            key_probe,
            value_probe,
            cosine,
            sine,
        ]
        if with_out:
            in_specs.append(spec((1, query_width, cut), lambda i: (layer, 0, late(i))))
            args.append(out_weight)
            out_shape.append(((group, model), bf))
            out_specs.append(spec((group, cut), lambda i: (0, late(i))))
        return pl.pallas_call(
            functools.partial(primal_kernel, CUTS, with_out),
            grid=(CUTS * (2 if with_out else 1),),
            in_specs=in_specs,
            out_specs=out_specs,
            out_shape=[jax.ShapeDtypeStruct(shape, kind) for shape, kind in out_shape],
            scratch_shapes=[
                pltpu.VMEM((group, query_width), f32),
                pltpu.VMEM((group, key_width), f32),
                pltpu.VMEM((group, key_width), f32),
            ],
            compiler_params=arbitrary,
            cost_estimate=cost(2 * group * model * query_width * 3, 16 << 20),
        )(*args)

    def moved_on(layer, kept, moved, blended_all, tangent_all):
        with_tangent = tangent_all is not None
        steps = CUTS if with_tangent else 1
        late = late_part(steps)
        queries, keys, values = kept
        in_specs = [
            smem,
            fixed(queries.shape),
            fixed(keys.shape),
            fixed(values.shape),
            fixed(moved.shape),
            table,
            table,
            spec((1, query_width, cut), lambda i: (layer, 0, late(i))),
            spec((rows_cut, query_width), lambda i: (late(i), 0)),
            spec((1, query_width, block), lambda i: (layer, 0, 0)),
        ]
        args = [
            group_lengths,
            queries,
            keys,
            values,
            moved,
            cosine,
            sine,
            out_weight,
            blended_all.reshape(rows_in_all, query_width),
            out_probe,
        ]
        if with_tangent:
            in_specs += [
                spec((group, cut), lambda i: (0, first_part(i))),
                *weight_specs(layer, first_part),
            ]
            args += [tangent_all.reshape(group, model), query_weight, key_full, value_full]
        return pl.pallas_call(
            functools.partial(tangent_kernel, steps, with_tangent),
            grid=(steps + CUTS,),
            in_specs=in_specs,
            out_specs=[
                spec((group, cut), lambda i: (0, late(i))),
                spec((rows_cut, block), lambda i: (late(i), 0)),
            ],
            out_shape=[
                jax.ShapeDtypeStruct((group, model), bf),
                jax.ShapeDtypeStruct((rows_in_all, block), bf),
            ],
            scratch_shapes=[
                pltpu.VMEM(moved.shape, f32),
                pltpu.VMEM((group, query_width), bf),
            ],
            compiler_params=arbitrary,
            cost_estimate=cost(2 * group * model * query_width * 3, 16 << 20),
        )(*args)

    def backward(layer, cotangent_all, kept):
        with_grad = layer > 0
        late = late_part(CUTS)
        queries, keys, values = kept
        sent = query_width + 2 * key_width
        in_specs = [
            smem,
            spec((group, cut), lambda i: (0, first_part(i))),
            spec((1, query_width, cut), lambda i: (layer, 0, first_part(i))),
            fixed(queries.shape),
            fixed(keys.shape),
            fixed(values.shape),
            table,
            table,
        ]
        args = [
            group_lengths,
            cotangent_all.reshape(group, model),
            out_weight,
            queries,
            keys,
            values,
            cosine,
            sine,
        ]
        out_shape = [jax.ShapeDtypeStruct((group, sent), bf)]
        out_specs = [fixed((group, sent))]
        if with_grad:
            in_specs += weight_specs(layer, late)
            args += [query_weight, key_full, value_full]
            out_shape.append(jax.ShapeDtypeStruct((group, model), bf))
            out_specs.append(spec((group, cut), lambda i: (0, late(i))))
        return pl.pallas_call(
            functools.partial(backward_kernel, CUTS, with_grad),
            grid=(CUTS * (2 if with_grad else 1),),
            in_specs=in_specs,
            out_specs=out_specs,
            out_shape=out_shape,
            scratch_shapes=[pltpu.VMEM((group, query_width), f32)],
            compiler_params=arbitrary,
            cost_estimate=cost(2 * group * model * query_width * 3, 16 << 20),
        )(*args)

    def products(per_layer):
        out_block = out_probe.shape[2]
        by_rows = query_width % (CUTS * HD) == 0
        blended_cut = query_width // CUTS if by_rows else query_width
        out_cut = out_block if by_rows else out_block // CUTS
        in_specs, args = [], []
        for number, (blocks, grads, blended, cotangents) in enumerate(per_layer):

            def place(i, j, number=number):
                return (0, jnp.clip((i - number) * CUTS + j, 0, CUTS - 1))

            def still(i, j):
                return (0, 0)

            in_specs += [
                pl.BlockSpec((rows_in_all, block // CUTS), place),
                pl.BlockSpec((rows_in_all, sent_width), still),
                pl.BlockSpec((rows_in_all, blended_cut), place if by_rows else still),
                pl.BlockSpec((rows_in_all, out_cut), still if by_rows else place),
            ]
            args += [
                blocks.reshape(rows_in_all, block),
                grads.reshape(rows_in_all, sent_width),
                blended.reshape(rows_in_all, query_width),
                cotangents.reshape(rows_in_all, out_block),
            ]
        shapes = [
            (block, query_width),
            (block, half_width),
            (block, half_width),
            (query_width, out_block),
        ]
        return pl.pallas_call(
            functools.partial(product_kernel, layers),
            grid=(layers, CUTS),
            in_specs=in_specs,
            out_specs=[
                pl.BlockSpec((1, rows // CUTS, columns), lambda i, j: (i, j, 0))
                for rows, columns in shapes[:3]
            ]
            + [
                pl.BlockSpec(
                    (1, blended_cut, out_cut),
                    lambda i, j: (i, j, 0) if by_rows else (i, 0, j),
                )
            ],
            out_shape=[
                jax.ShapeDtypeStruct((layers, rows, columns), f32) for rows, columns in shapes
            ],
            compiler_params=pltpu.CompilerParams(
                dimension_semantics=("arbitrary", "arbitrary")
            ),
            cost_estimate=cost(2 * rows_in_all * block * query_width * 4, 32 << 20),
        )(*args)

    slots = (width, share, model)
    probe_slots = (batches, width, share, block)

    whole0, blocks0 = communicate(
        open_kernel,
        sizes,
        0,
        [tokens, gains[0]],
        [whole_shape, blocks_shape],
        [shard_shape, pieces_shape, pieces_shape],
    )
    queries, keys, values, blended0, partial, out = primal(
        0, whole0.reshape(group, model), blocks0.reshape(rows_in_all, block)
    )
    kept0 = (queries, keys, values)
    stream1, whole1, blocks1, moved, blended_all0 = communicate(
        second_kernel,
        sizes,
        1,
        [out.reshape(slots), tokens, gains[1], partial.reshape(back_shape), blended0],
        [
            (shard_shape, bf),
            whole_shape,
            blocks_shape,
            ((group, sent_width), f32),
            ((batches, group, query_width), bf),
        ],
        [sum_shape, sum_shape, sum_shape, shard_shape, pieces_shape, pieces_shape, back_shape],
    )
    terms, probed = moved_on(0, kept0, join_moved(moved), blended_all0, None)
    queries, keys, values, blended1, partial = primal(
        1, whole1.reshape(group, model), blocks1.reshape(rows_in_all, block)
    )
    kept1 = (queries, keys, values)
    sums = [sum_shape, sum_shape, sum_shape, probe_shape, probe_shape, probe_shape]
    tangent, tangent_all, moved, blended_all1 = communicate(
        third_kernel,
        sizes,
        2,
        [
            terms.reshape(slots),
            probed.reshape(probe_slots),
            stream1,
            gains[1],
            partial.reshape(back_shape),
            blended1,
        ],
        [
            (shard_shape, f32),
            whole_shape,
            ((group, sent_width), f32),
            ((batches, group, query_width), bf),
        ],
        sums + [shard_shape, pieces_shape, pieces_shape, back_shape],
    )
    terms, probed = moved_on(1, kept1, join_moved(moved), blended_all1, tangent_all)
    cotangent, cotangent_all, cotangents1 = communicate(
        fourth_kernel,
        sizes,
        3,
        [terms.reshape(slots), probed.reshape(probe_slots), tangent, row_mask],
        [(shard_shape, f32), whole_shape, blocks_shape],
        sums + [shard_shape, pieces_shape, pieces_shape, pieces_shape, pieces_shape],
    )
    grads1, terms = backward(1, cotangent_all, kept1)
    _, cotangent_all, cotangents0, grads_all1 = communicate(
        fifth_kernel,
        sizes,
        4,
        [terms.reshape(slots), stream1, gains[1], cotangent, to_send(grads1)],
        [
            (shard_shape, f32),
            whole_shape,
            blocks_shape,
            ((batches, group, sent_width), bf),
        ],
        [sum_shape, sum_shape, sum_shape, shard_shape, pieces_shape, pieces_shape],
    )
    (grads0,) = backward(0, cotangent_all, kept0)
    (grads_all0,) = communicate(
        last_kernel,
        sizes,
        5,
        [to_send(grads0)],
        [((batches, group, sent_width), bf)],
        [],
    )
    return tuple(
        products(
            [
                (blocks0, grads_all0, blended_all0, cotangents0),
                (blocks1, grads_all1, blended_all1, cotangents1),
            ]
        )
    )


def solution(mesh):
    placed = (
        P(("dp", "tensor"), None),
        P(),
        P(),
        P(None, None, "tensor"),
        P(None, None, "tensor"),
        P(None, None, "tensor"),
        P(None, "tensor", None),
        P(None, "dp", "tensor"),
        P(None, "dp", "tensor"),
        P(None, "dp", "tensor"),
        P(None, "tensor", "dp"),
    )
    return jax.shard_map(
        body,
        mesh=mesh,
        in_specs=placed,
        out_specs=(
            P(None, "dp", "tensor"),
            P(None, "dp", "tensor"),
            P(None, "dp", "tensor"),
            P(None, "tensor", "dp"),
        ),
        check_vma=False,
    )
```

profile of v0, /device:TPU:0, one launch (start us, length us, event | category | flops | bytes accessed | tf_op | source)
XLA Modules:
  0.0 479.6 jit_solution(18011055081070174701)
XLA Ops:
  0.6 1.3 dynamic_slice.5.lengths
  2.0 1.3 fusion.5.mask
  3.3 1.5 fusion.7
  4.7 0.5 fusion
  5.3 0.9 pad_maximum_fusion
  6.1 35.3 %shard_map.138 = (bf16[8,32,4096]{2,1,0:T(8,128)(2,1)}, bf16[4,8,32,1024]{3,2,1,0:T(8,128)(2,1)}) custom-call(bf16[32,4096]{1,0:T(8,128)(2,1)} %tokens.3, f32[1,4096]{1,0:T(1,128)} %get-tuple-element.73.gain), custom_call_target="tpu_custom_call" | custom-call | tf_op jit(solution)/shard_map/pallas_call | solution.py:441
  41.4 15.3 %shard_map.139 = (bf16[256,512]{1,0:T(8,128)(2,1)}, bf16[256,128]{1,0:T(8,128)(2,1)}, bf16[256,128]{1,0:T(8,128)(2,1)}, bf16[256,512]{1,0:T(8,128)(2,1)}, bf16[1...) custom-call(s32[1]{0:T(128)} %dynamic_slice.5.lengths, bf16[256,4096]{1,0:T(8,128)(2,1)} %bitcast.35, ...), custom_call_target="tpu_custom_call" | custom-call | flops 3221225472 | bytes 16777216 | tf_op jit(solution)/shard_map/pallas_call | solution.py:862
  56.8 79.8 %shard_map.140 = (bf16[32,4096]{1,0:T(8,128)(2,1)}, bf16[8,32,4096]{2,1,0:T(8,128)(2,1)}, bf16[4,8,32,1024]{3,2,1,0:T(8,128)(2,1)}, f32[256,768]{1,0:T(8,128)}, bf16[4,256,512]{2,1,0:T(8,128)(2,1)}) custom-call(bf16[8,32,4096]{2,1,0:T(8,128)(2,1)} %bitcast.30, bf16[32,4096]{1,0:T(8,128)(2,1)} %tokens.3, f32[1,4096]{1,0:T(1,128)} %get-tuple-element.72.gain, ...), custom_call_target="tpu_custom_call" | custom-call | tf_op jit(solution)/shard_map/pallas_call | solution.py:441
  136.6 11.1 %shard_map.141 = (bf16[256,512]{1,0:T(8,128)(2,1)}, bf16[256,128]{1,0:T(8,128)(2,1)}, bf16[256,128]{1,0:T(8,128)(2,1)}, bf16[256,512]{1,0:T(8,128)(2,1)}, bf16[1024,768]{1,0:T(8,128)(2,1)}) custom-call(s32[1]{0:T(128)} %dynamic_slice.5.lengths, bf16[256,4096]{1,0:T(8,128)(2,1)} %bitcast.24, bf16[2,4096,512]{2,1,0:T(8,128)(2,1)} %rest_0_.3, ...), custom_call_target="tpu_custom_call" | custom-call | flops 3221225472 | bytes 16777216 | tf_op jit(solution)/shard_map/pallas_call | solution.py:862
  147.7 9.8 %shard_map.142 = (bf16[256,4096]{1,0:T(8,128)(2,1)}, bf16[1024,1024]{1,0:T(8,128)(2,1)}) custom-call(s32[1]{0:T(128)} %dynamic_slice.5.lengths, bf16[256,512]{1,0:T(8,128)(2,1)} %get-tuple-element.48.queries, bf16[256,128]{1,0:T(8,128)(2,1)} %get-tuple-element.49.keys, bf16[256,128]{1,0:T(8,128)(2,1)} %get-tuple-element.50.values, ...), custom_call_target="tpu_custom_call" | custom-call | flops 3221225472 | bytes 16777216 | tf_op jit(solution)/shard_map/pallas_call | solution.py:912
  157.5 82.1 %shard_map.143 = (f32[32,4096]{1,0:T(8,128)}, bf16[8,32,4096]{2,1,0:T(8,128)(2,1)}, f32[256,768]{1,0:T(8,128)}, bf16[4,256,512]{2,1,0:T(8,128)(2,1)}) custom-call(bf16[8,32,4096]{2,1,0:T(8,128)(2,1)} %bitcast.27, bf16[4,8,32,1024]{3,2,1,0:T(8,128)(2,1)} %bitcast.28, bf16[32,4096]{1,0:T(8,128)(2,1)} %get-tuple-element.55.stream_in, ...), custom_call_target="tpu_custom_call" | custom-call | tf_op jit(solution)/shard_map/pallas_call | solution.py:441
  239.6 15.0 %shard_map.144 = (bf16[256,4096]{1,0:T(8,128)(2,1)}, bf16[1024,1024]{1,0:T(8,128)(2,1)}) custom-call(s32[1]{0:T(128)} %dynamic_slice.5.lengths, bf16[256,512]{1,0:T(8,128)(2,1)} %get-tuple-element.45.queries, bf16[256,128]{1,0:T(8,128)(2,1)} %get-tuple-element.46.keys, bf16[256,128]{1,0:T(8,128)(2,1)} %get-tuple-element.47.values, ...), custom_call_target="tpu_custom_call" | custom-call | flops 3221225472 | bytes 16777216 | tf_op jit(solution)/shard_map/pallas_call | solution.py:912
  254.6 72.2 %shard_map.145 = (f32[32,4096]{1,0:T(8,128)}, bf16[8,32,4096]{2,1,0:T(8,128)(2,1)}, bf16[4,8,32,1024]{3,2,1,0:T(8,128)(2,1)}) custom-call(bf16[8,32,4096]{2,1,0:T(8,128)(2,1)} %bitcast.31, bf16[4,8,32,1024]{3,2,1,0:T(8,128)(2,1)} %bitcast.32, f32[32,4096]{1,0:T(8,128)} %get-tuple-element.63.tangent, f32[32,1]{1,0:T(8,128)} %fusion.5.mask), custom_call_target="tpu_custom_call" | custom-call | tf_op jit(solution)/shard_map/pallas_call | solution.py:441
  326.9 13.6 %shard_map.146 = (bf16[256,768]{1,0:T(8,128)(2,1)}, bf16[256,4096]{1,0:T(8,128)(2,1)}) custom-call(s32[1]{0:T(128)} %dynamic_slice.5.lengths, bf16[256,4096]{1,0:T(8,128)(2,1)} %bitcast.25, bf16[2,512,4096]{2,1,0:T(8,128)(2,1)} %out_weight.7, bf16[256,512]{1,0:T(8,128)(2,1)} %get-tuple-element.45.queries, bf16[256,128]{1,0:T(8,128)(2,1)} %get-tuple-element.46.keys, ...), custom_call_target="tpu_custom_call" | custom-call | flops 3221225472 | bytes 16777216 | tf_op jit(solution)/shard_map/pallas_call | solution.py:964
  340.4 76.9 %shard_map.147 = (f32[32,4096]{1,0:T(8,128)}, bf16[8,32,4096]{2,1,0:T(8,128)(2,1)}, bf16[4,8,32,1024]{3,2,1,0:T(8,128)(2,1)}, bf16[4,256,768]{2,1,0:T(8,128)(2,1)}) custom-call(bf16[8,32,4096]{2,1,0:T(8,128)(2,1)} %bitcast.29, bf16[32,4096]{1,0:T(8,128)(2,1)} %get-tuple-element.55.stream_in, f32[1,4096]{1,0:T(1,128)} %get-tuple-element.72.gain, ...), custom_call_target="tpu_custom_call" | custom-call | tf_op jit(solution)/shard_map/pallas_call | solution.py:441
  417.4 8.0 %shard_map.148.grads = bf16[256,768]{1,0:T(8,128)(2,1)} custom-call(s32[1]{0:T(128)} %dynamic_slice.5.lengths, bf16[256,4096]{1,0:T(8,128)(2,1)} %bitcast.45, bf16[2,512,4096]{2,1,0:T(8,128)(2,1)} %out_weight.7, bf16[256,512]{1,0:T(8,128)(2,1)} %get-tuple-element.48.queries, bf16[256,128]{1,0:T(8,128)(2,1)} %get-tuple-element.49.keys, ...), custom_call_target="tpu_custom_call" | custom-call | flops 3221225472 | bytes 16777216 | tf_op jit(solution)/shard_map/pallas_call | solution.py:964
  425.4 39.9 %shard_map.149 = bf16[4,256,768]{2,1,0:T(8,128)(2,1)} custom-call(bf16[256,768]{1,0:T(8,128)(2,1)} %shard_map.148.grads), custom_call_target="tpu_custom_call" | custom-call | tf_op jit(solution)/shard_map/pallas_call | solution.py:441
  465.3 14.2 %shard_map.150 = (f32[2,1024,512]{2,1,0:T(8,128)}, f32[2,1024,128]{2,1,0:T(8,128)}, f32[2,1024,128]{2,1,0:T(8,128)}, f32[2,512,1024]{2,1,0:T(8,128)}) custom-call(bf16[1024,1024]{1,0:T(8,128)(2,1)} %bitcast.34, bf16[1024,768]{1,0:T(8,128)(2,1)} %bitcast.38, bf16[1024,512]{1,0:T(8,128)(2,1)} %bitcast.40, bf16[1024,1024]{1,0:T(8,128)(2,1)} %bitcast.44, ...), custom_call_target="tpu_custom_call" | custom-call | flops 4294967296 | bytes 33554432 | tf_op jit(solution)/shard_map/pallas_call | solution.py:1007
  (2 shorter events, 0.0 us)
where the time goes:
time: 486 us; the launch traced here: 480 us
  Pallas kernels  473 us (97%)
    pallas_call x6, Pallas kernels, communicate(): pl.pallas_call(functools.partial(kernel, sizes), out_shape=[jax.ShapeDtyp...  386 us
    pallas_call x2, Pallas kernels, primal(): pl.pallas_call(functools.partial(primal_kernel, CUTS, with_out), grid=(CU...  26.5 us
    pallas_call x2, Pallas kernels, moved_on(): pl.pallas_call(functools.partial(tangent_kernel, steps, with_tangent), gr...  24.9 us
    pallas_call x2, Pallas kernels, backward(): pl.pallas_call(functools.partial(backward_kernel, CUTS, with_grad), grid=...  21.6 us
    pallas_call x1, Pallas kernels, products(): pl.pallas_call(functools.partial(product_kernel, layers), grid=(layers, C...  14.2 us

commit v1 on v0

--- a/solution.py
+++ b/solution.py
@@ -64,7 +64,7 @@
 
 def semaphore_count(sizes):
     batches, width = sizes
-    return 4 * width + 3 * batches
+    return 4 * width + 6 * batches
 
 
 class Fabric:
@@ -75,6 +75,7 @@
         self.col = lax.axis_index("tensor")
         self.send, self.recv, self.used = send, recv, 0
         self.pending = []
+        self.guarded = []
 
     def copy(self, source, target, row, col):
         number = self.used
@@ -95,6 +96,8 @@
     def drain(self):
         for made in self.pending:
             made.wait_send()
+        for condition, made in self.guarded:
+            pl.when(condition)(made.wait_send)
 
     def mate(self):
         return flip(self.col, 1)
@@ -182,21 +185,111 @@
 
         return finish
 
-    def scatter_batch(self, source, landed, steps):
-        return [
-            self.copy(
-                source.at[self.batch(step)], landed.at[step], self.batch(step), self.col
+    def reserve(self, count):
+        first = self.used
+        self.used += count
+        assert self.used <= semaphore_count((self.batches, self.width))
+        return first
+
+    def hop(self, source, target, number, way):
+        return pltpu.make_async_remote_copy(
+            src_ref=source,
+            dst_ref=target,
+            send_sem=self.send.at[number],
+            recv_sem=self.recv.at[number],
+            device_id=(jnp.clip(self.row + way, 0, self.batches - 1), self.col),
+            device_id_type=MESH,
+        )
+
+    def rank(self, way):
+        return self.row if way > 0 else self.batches - 1 - self.row
+
+
+class GatherChain:
+    def __init__(self, fabric, source, target):
+        self.fabric, self.source, self.target = fabric, source, target
+        self.first = fabric.reserve(2 * (fabric.batches - 1))
+        target[fabric.row] = source[...]
+
+    def number(self, way, step):
+        return self.first + (0 if way > 0 else self.fabric.batches - 1) + step - 1
+
+    def arrive(self, step):
+        fabric = self.fabric
+        for way in (1, -1):
+            piece = jnp.clip(fabric.row - way * step, 0, fabric.batches - 1)
+            made = fabric.hop(
+                self.target.at[piece], self.target.at[piece], self.number(way, step), way
             )
-            for step in steps
-        ]
-
-    def gather_batch(self, source, target):
-        made = [
-            self.copy(source, target.at[self.row], self.batch(step), self.col)
-            for step in range(1, self.batches)
-        ]
-        target[self.row] = source[...]
-        return made
+            pl.when(fabric.rank(way) >= step)(made.wait_recv)
+
+    def step(self, step):
+        fabric = self.fabric
+        if step > 1:
+            self.arrive(step - 1)
+        for way in (1, -1):
+            piece = jnp.clip(fabric.row - way * (step - 1), 0, fabric.batches - 1)
+            source = self.source if step == 1 else self.target.at[piece]
+            made = fabric.hop(source, self.target.at[piece], self.number(way, step), way)
+            rank = fabric.rank(way)
+            condition = (rank >= step - 1) & (rank < fabric.batches - 1)
+            pl.when(condition)(made.start)
+            fabric.guarded.append((condition, made))
+
+    def finish(self):
+        self.arrive(self.fabric.batches - 1)
+
+
+class ScatterChain:
+    def __init__(self, fabric, source, landed, leaving):
+        self.fabric, self.source = fabric, source
+        self.landed, self.leaving = landed, leaving
+        self.first = fabric.reserve(2 * (fabric.batches - 1))
+
+    def hop(self, source, way, step):
+        side = 0 if way > 0 else 1
+        number = self.first + side * (self.fabric.batches - 1) + step - 1
+        return self.fabric.hop(source, self.landed.at[side, step - 1], number, way)
+
+    def step(self, step):
+        fabric = self.fabric
+        last = fabric.batches - 1
+        for way in (1, -1):
+            side = 0 if way > 0 else 1
+            rank = fabric.rank(way)
+            goal = jnp.clip(fabric.batches + rank - step, 0, last)
+            goal = goal if way > 0 else last - goal
+            own = self.hop(self.source.at[goal], way, step)
+            pl.when(rank == 0)(own.start)
+            fabric.guarded.append((rank == 0, own))
+            if step > 1:
+                buffer = self.leaving.at[side, step - 1]
+                summed = self.hop(buffer, way, step)
+                before = self.hop(buffer, way, step - 1)
+                condition = (rank > 0) & (rank < step)
+
+                @pl.when(condition)
+                def _():
+                    before.wait_recv()
+                    buffer[...] = low(
+                        wide(self.source[goal]) + wide(self.landed[side, step - 2])
+                    )
+                    summed.start()
+
+                fabric.guarded.append((condition, summed))
+
+    def finish(self, total):
+        fabric = self.fabric
+        last = fabric.batches - 1
+        total[...] = wide(self.source[fabric.row])
+        for way in (1, -1):
+            side = 0 if way > 0 else 1
+            made = self.hop(self.source.at[fabric.row], way, last)
+
+            @pl.when(fabric.rank(way) > 0)
+            def _():
+                made.wait_recv()
+                total[...] += wide(self.landed[side, last - 1])
 
 
 def inverse_of(stream):
@@ -211,7 +304,12 @@
         pieces[number] = rounded[:, number * block : (number + 1) * block]
 
 
-def gather_both(fabric, shard, pieces, exchanged, whole, blocks):
+def open_kernel(sizes, tokens, gain, whole, blocks, shard, pieces, exchanged, send, recv):
+    fabric = Fabric(sizes, send, recv)
+    ready = fabric.greet()
+    stream = wide(tokens[...])
+    set_shard(stream * inverse_of(stream) * gain[...], shard, pieces)
+    ready()
     arrived = fabric.exchange(pieces, exchanged)
     forward, finish = fabric.gather(shard, lambda col: whole.at[col])
     arrived()
@@ -220,23 +318,6 @@
     forward_blocks()
     finish()
     finish_blocks()
-
-
-def add_landed(own, landed, copies, steps):
-    total = wide(own)
-    for made, step in zip(copies, steps):
-        made.wait_recv()
-        total = total + wide(landed[step])
-    return total
-
-
-def open_kernel(sizes, tokens, gain, whole, blocks, shard, pieces, exchanged, send, recv):
-    fabric = Fabric(sizes, send, recv)
-    ready = fabric.greet()
-    stream = wide(tokens[...])
-    set_shard(stream * inverse_of(stream) * gain[...], shard, pieces)
-    ready()
-    gather_both(fabric, shard, pieces, exchanged, whole, blocks)
     fabric.drain()
 
 
@@ -259,44 +340,41 @@
     pieces,
     exchanged,
     returned,
+    leaving,
     send,
     recv,
 ):
     fabric = Fabric(sizes, send, recv)
+    back = ScatterChain(fabric, partial, returned, leaving)
+    fetch = GatherChain(fabric, blended, blended_all)
     fabric.greet()()
     slot = lambda col: terms.at[col]
     paired = fabric.pair_up(slot, beside)
-    steps = list(range(1, fabric.batches))
-    back = fabric.scatter_batch(partial, returned, steps)
+    back.step(1)
+    fetch.step(1)
     total = fabric.spread(slot, paired, beside, summed, landed)()
     rounded = low(wide(tokens[...]) + total)
     stream_out[...] = rounded
     stream = wide(rounded)
     set_shard(stream * inverse_of(stream) * gain[...], shard, pieces)
-    gather_both(fabric, shard, pieces, exchanged, whole, blocks)
-    fetched = fabric.gather_batch(blended, blended_all)
-    moved[...] = add_landed(partial[fabric.row], returned, back, steps)
-    for made in fetched:
-        made.wait_recv()
+    arrived = fabric.exchange(pieces, exchanged)
+    forward, finish = fabric.gather(shard, lambda col: whole.at[col])
+    steps = list(range(2, fabric.batches))
+    for step in steps[:-1]:
+        back.step(step)
+        fetch.step(step)
+    arrived()
+    forward_blocks, finish_blocks = fabric.gather(exchanged, lambda col: blocks.at[:, col])
+    forward()
+    for step in steps[-1:]:
+        back.step(step)
+        fetch.step(step)
+    forward_blocks()
+    finish()
+    finish_blocks()
+    back.finish(moved)
+    fetch.finish()
     fabric.drain()
-
-
-def tangent_total(fabric, terms, probed, beside, summed, landed, probe_bufs, pieces, exchanged):
-    beside_p, summed_p, landed_p = probe_bufs
-    slot = lambda col: terms.at[col]
-    slot_p = lambda col: probed.at[:, col]
-    paired_p = fabric.pair_up(slot_p, beside_p)
-    paired = fabric.pair_up(slot, beside)
-    finish_p = fabric.spread(slot_p, paired_p, beside_p, summed_p, landed_p)
-    finish = fabric.spread(slot, paired, beside, summed, landed)
-    pieces[...] = low(finish_p())
-    total = finish()
-    fabric.exchange(pieces, exchanged)()
-    block = pieces.shape[-1]
-    return [
-        total[:, number * block : (number + 1) * block] + wide(exchanged[number])
-        for number in range(fabric.batches)
-    ]
 
 
 def third_kernel(
@@ -321,20 +399,29 @@
     pieces,
     exchanged,
     returned,
+    leaving,
     send,
     recv,
 ):
     fabric = Fabric(sizes, send, recv)
+    back = ScatterChain(fabric, partial, returned, leaving)
+    fetch = GatherChain(fabric, blended, blended_all)
     fabric.greet()()
-    steps = list(range(1, fabric.batches))
-    early = steps[: (len(steps) + 1) // 2]
-    back = fabric.scatter_batch(partial, returned, early)
-    parts = tangent_total(
-        fabric, terms, probed, beside, summed, landed, (beside_p, summed_p, landed_p),
-        pieces, exchanged,
-    )
-    back += fabric.scatter_batch(partial, returned, steps[len(early) :])
-    change = jnp.concatenate(parts, axis=-1)
+    slot = lambda col: terms.at[col]
+    slot_p = lambda col: probed.at[:, col]
+    paired_p = fabric.pair_up(slot_p, beside_p)
+    paired = fabric.pair_up(slot, beside)
+    back.step(1)
+    fetch.step(1)
+    finish_p = fabric.spread(slot_p, paired_p, beside_p, summed_p, landed_p)
+    finish = fabric.spread(slot, paired, beside, summed, landed)
+    pieces[...] = low(finish_p())
+    arrived = fabric.exchange(pieces, exchanged)
+    steps = list(range(2, fabric.batches))
+    for step in steps[:-1]:
+        back.step(step)
+        fetch.step(step)
+    change = joined(finish(), arrived, exchanged)
     tangent[...] = change
     stream = wide(stream_in[...])
     inverse = inverse_of(stream)
@@ -342,14 +429,27 @@
     shard[...] = low(
         gain[...] * (change * inverse - stream * inverse * inverse * inverse * shift)
     )
-    fetched = fabric.gather_batch(blended, blended_all)
     forward, finish = fabric.gather(shard, lambda col: whole.at[col])
+    for step in steps[-1:]:
+        back.step(step)
+        fetch.step(step)
     forward()
     finish()
-    moved[...] = add_landed(partial[fabric.row], returned, back, steps)
-    for made in fetched:
-        made.wait_recv()
+    back.finish(moved)
+    fetch.finish()
     fabric.drain()
+
+
+def joined(total, arrived, exchanged):
+    arrived()
+    block = exchanged.shape[-1]
+    return jnp.concatenate(
+        [
+            total[:, number * block : (number + 1) * block] + wide(exchanged[number])
+            for number in range(exchanged.shape[0])
+        ],
+        axis=-1,
+    )
 
 
 def fourth_kernel(
@@ -360,7 +460,7 @@
     mask,
     cotangent,
     whole,
-    blocks,
+    pieces_out,
     beside,
     summed,
     landed,
@@ -370,22 +470,26 @@
     shard,
     pieces,
     exchanged,
-    pieces_p,
-    exchanged_p,
     send,
     recv,
 ):
     fabric = Fabric(sizes, send, recv)
     fabric.greet()()
-    parts = tangent_total(
-        fabric, terms, probed, beside, summed, landed, (beside_p, summed_p, landed_p),
-        pieces_p, exchanged_p,
-    )
-    change = jnp.concatenate(parts, axis=-1)
+    slot = lambda col: terms.at[col]
+    slot_p = lambda col: probed.at[:, col]
+    paired_p = fabric.pair_up(slot_p, beside_p)
+    paired = fabric.pair_up(slot, beside)
+    finish_p = fabric.spread(slot_p, paired_p, beside_p, summed_p, landed_p)
+    finish = fabric.spread(slot, paired, beside, summed, landed)
+    pieces[...] = low(finish_p())
+    arrived = fabric.exchange(pieces, exchanged)
+    change = joined(finish(), arrived, exchanged)
     result = mask[...] * (tangent[...] + change)
     cotangent[...] = result
-    set_shard(result, shard, pieces)
-    gather_both(fabric, shard, pieces, exchanged, whole, blocks)
+    set_shard(result, shard, pieces_out)
+    forward, finish = fabric.gather(shard, lambda col: whole.at[col])
+    forward()
+    finish()
     fabric.drain()
 
 
@@ -396,43 +500,65 @@
     gain,
     cotangent,
     grads,
-    cotangent_out,
+    pieces_in,
     whole,
     blocks,
     grads_all,
+    pieces_out,
     beside,
     summed,
     landed,
     shard,
-    pieces,
     exchanged,
     send,
     recv,
 ):
     fabric = Fabric(sizes, send, recv)
+    fetch = GatherChain(fabric, grads, grads_all)
     fabric.greet()()
     slot = lambda col: terms.at[col]
     paired = fabric.pair_up(slot, beside)
+    arrived = fabric.exchange(pieces_in, exchanged)
+    fetch.step(1)
     total = fabric.spread(slot, paired, beside, summed, landed)()
     stream = wide(stream_in[...])
     inverse = inverse_of(stream)
     scaled = total * gain[...]
     shift = jnp.mean(stream * scaled, axis=-1, keepdims=True)
     result = cotangent[...] + inverse * (scaled - stream * inverse * inverse * shift)
-    cotangent_out[...] = result
-    set_shard(result, shard, pieces)
-    gather_both(fabric, shard, pieces, exchanged, whole, blocks)
-    fetched = fabric.gather_batch(grads, grads_all)
-    for made in fetched:
-        made.wait_recv()
+    set_shard(result, shard, pieces_out)
+    forward, finish = fabric.gather(shard, lambda col: whole.at[col])
+    arrived()
+    forward_blocks, finish_blocks = fabric.gather(exchanged, lambda col: blocks.at[:, col])
+    steps = list(range(2, fabric.batches))
+    for step in steps[:-1]:
+        fetch.step(step)
+    forward()
+    for step in steps[-1:]:
+        fetch.step(step)
+    forward_blocks()
+    finish()
+    finish_blocks()
+    fetch.finish()
     fabric.drain()
 
 
-def last_kernel(sizes, grads, grads_all, send, recv):
+def last_kernel(sizes, grads, pieces_in, grads_all, blocks, exchanged, send, recv):
     fabric = Fabric(sizes, send, recv)
-    fabric.greet(along_tensor=False)()
-    for made in fabric.gather_batch(grads, grads_all):
-        made.wait_recv()
+    fetch = GatherChain(fabric, grads, grads_all)
+    fabric.greet()()
+    arrived = fabric.exchange(pieces_in, exchanged)
+    fetch.step(1)
+    arrived()
+    forward_blocks, finish_blocks = fabric.gather(exchanged, lambda col: blocks.at[:, col])
+    steps = list(range(2, fabric.batches))
+    for step in steps[:-1]:
+        fetch.step(step)
+    forward_blocks()
+    for step in steps[-1:]:
+        fetch.step(step)
+    finish_blocks()
+    fetch.finish()
     fabric.drain()
 
 
@@ -782,6 +908,7 @@
     sum_shape = (chips, share, model)
     probe_shape = (chips, batches, share, block)
     back_shape = (batches, group, sent_width)
+    chain_shape = (2, batches - 1, group, sent_width)
     rows_in_all = batches * group
     gains = [norm_gains[number][None] for number in range(layers)]
     cut = model // CUTS
@@ -1054,7 +1181,7 @@
             ((group, sent_width), f32),
             ((batches, group, query_width), bf),
         ],
-        [sum_shape, sum_shape, sum_shape, shard_shape, pieces_shape, pieces_shape, back_shape],
+        [sum_shape, sum_shape, sum_shape, shard_shape, pieces_shape, pieces_shape, chain_shape, chain_shape],
     )
     terms, probed = moved_on(0, kept0, join_moved(moved), blended_all0, None)
     queries, keys, values, blended1, partial = primal(
@@ -1080,39 +1207,46 @@
             ((group, sent_width), f32),
             ((batches, group, query_width), bf),
         ],
-        sums + [shard_shape, pieces_shape, pieces_shape, back_shape],
+        sums + [shard_shape, pieces_shape, pieces_shape, chain_shape, chain_shape],
     )
     terms, probed = moved_on(1, kept1, join_moved(moved), blended_all1, tangent_all)
-    cotangent, cotangent_all, cotangents1 = communicate(
+    cotangent, cotangent_all, cotangent_pieces = communicate(
         fourth_kernel,
         sizes,
         3,
         [terms.reshape(slots), probed.reshape(probe_slots), tangent, row_mask],
-        [(shard_shape, f32), whole_shape, blocks_shape],
-        sums + [shard_shape, pieces_shape, pieces_shape, pieces_shape, pieces_shape],
+        [(shard_shape, f32), whole_shape, (pieces_shape, bf)],
+        sums + [shard_shape, pieces_shape, pieces_shape],
     )
     grads1, terms = backward(1, cotangent_all, kept1)
-    _, cotangent_all, cotangents0, grads_all1 = communicate(
+    cotangent_all, cotangents1, grads_all1, cotangent_pieces = communicate(
         fifth_kernel,
         sizes,
         4,
-        [terms.reshape(slots), stream1, gains[1], cotangent, to_send(grads1)],
         [
-            (shard_shape, f32),
+            terms.reshape(slots),
+            stream1,
+            gains[1],
+            cotangent,
+            to_send(grads1),
+            cotangent_pieces,
+        ],
+        [
             whole_shape,
             blocks_shape,
             ((batches, group, sent_width), bf),
+            (pieces_shape, bf),
         ],
-        [sum_shape, sum_shape, sum_shape, shard_shape, pieces_shape, pieces_shape],
+        [sum_shape, sum_shape, sum_shape, shard_shape, pieces_shape],
     )
     (grads0,) = backward(0, cotangent_all, kept0)
-    (grads_all0,) = communicate(
+    grads_all0, cotangents0 = communicate(
         last_kernel,
         sizes,
         5,
-        [to_send(grads0)],
-        [((batches, group, sent_width), bf)],
-        [],
+        [to_send(grads0), cotangent_pieces],
+        [((batches, group, sent_width), bf), blocks_shape],
+        [pieces_shape],
     )
     return tuple(
         products(

time: 486 us -> 378 us (0.78); the launches traced: 480 us -> 377 us
  Pallas kernels: 473 us -> 371 us
    pallas_call x6, Pallas kernels: 386 us -> 284 us  [communicate(): pl.pallas_call(functools.partial(kernel, sizes), out_shape=[jax.ShapeDtyp...]
where the time goes in v1:
time: 378 us; the launch traced here: 377 us
  Pallas kernels  371 us (98%)
    pallas_call x6, Pallas kernels, communicate(): pl.pallas_call(functools.partial(kernel, sizes), out_shape=[jax.ShapeDtyp...  284 us
    pallas_call x2, Pallas kernels, primal(): pl.pallas_call(functools.partial(primal_kernel, CUTS, with_out), grid=(CU...  26.4 us
    pallas_call x2, Pallas kernels, moved_on(): pl.pallas_call(functools.partial(tangent_kernel, steps, with_tangent), gr...  24.6 us
    pallas_call x2, Pallas kernels, backward(): pl.pallas_call(functools.partial(backward_kernel, CUTS, with_grad), grid=...  21.5 us
    pallas_call x1, Pallas kernels, products(): pl.pallas_call(functools.partial(product_kernel, layers), grid=(layers, C...  14.2 us

profile of v1, /device:TPU:0, one launch (start us, length us, event | category | flops | bytes accessed | tf_op | source)
XLA Modules:
  0.0 376.8 jit_solution(11634079755023518166)
XLA Ops:
  0.6 1.3 dynamic_slice.5.lengths
  1.9 1.2 fusion.5.mask
  3.2 1.5 fusion.7
  4.6 0.5 fusion
  5.2 0.8 pad_maximum_fusion
  6.0 35.5 %shard_map.138 = (bf16[8,32,4096]{2,1,0:T(8,128)(2,1)}, bf16[4,8,32,1024]{3,2,1,0:T(8,128)(2,1)}) custom-call(bf16[32,4096]{1,0:T(8,128)(2,1)} %tokens.3, f32[1,4096]{1,0:T(1,128)} %get-tuple-element.79.gain), custom_call_target="tpu_custom_call" | custom-call | tf_op jit(solution)/shard_map/pallas_call | solution.py:567
  41.6 15.3 %shard_map.139 = (bf16[256,512]{1,0:T(8,128)(2,1)}, bf16[256,128]{1,0:T(8,128)(2,1)}, bf16[256,128]{1,0:T(8,128)(2,1)}, bf16[256,512]{1,0:T(8,128)(2,1)}, bf16[1...) custom-call(s32[1]{0:T(128)} %dynamic_slice.5.lengths, bf16[256,4096]{1,0:T(8,128)(2,1)} %bitcast.35, ...), custom_call_target="tpu_custom_call" | custom-call | flops 3221225472 | bytes 16777216 | tf_op jit(solution)/shard_map/pallas_call | solution.py:989
  56.9 54.5 %shard_map.140 = (bf16[32,4096]{1,0:T(8,128)(2,1)}, bf16[8,32,4096]{2,1,0:T(8,128)(2,1)}, bf16[4,8,32,1024]{3,2,1,0:T(8,128)(2,1)}, f32[256,768]{1,0:T(8,128)}, bf16[4,256,512]{2,1,0:T(8,128)(2,1)}) custom-call(bf16[8,32,4096]{2,1,0:T(8,128)(2,1)} %bitcast.30, bf16[32,4096]{1,0:T(8,128)(2,1)} %tokens.3, f32[1,4096]{1,0:T(1,128)} %get-tuple-element.78.gain, ...), custom_call_target="tpu_custom_call" | custom-call | tf_op jit(solution)/shard_map/pallas_call | solution.py:567
  111.4 11.1 %shard_map.141 = (bf16[256,512]{1,0:T(8,128)(2,1)}, bf16[256,128]{1,0:T(8,128)(2,1)}, bf16[256,128]{1,0:T(8,128)(2,1)}, bf16[256,512]{1,0:T(8,128)(2,1)}, bf16[1024,768]{1,0:T(8,128)(2,1)}) custom-call(s32[1]{0:T(128)} %dynamic_slice.5.lengths, bf16[256,4096]{1,0:T(8,128)(2,1)} %bitcast.24, bf16[2,4096,512]{2,1,0:T(8,128)(2,1)} %rest_0_.3, ...), custom_call_target="tpu_custom_call" | custom-call | flops 3221225472 | bytes 16777216 | tf_op jit(solution)/shard_map/pallas_call | solution.py:989
  122.4 9.8 %shard_map.142 = (bf16[256,4096]{1,0:T(8,128)(2,1)}, bf16[1024,1024]{1,0:T(8,128)(2,1)}) custom-call(s32[1]{0:T(128)} %dynamic_slice.5.lengths, bf16[256,512]{1,0:T(8,128)(2,1)} %get-tuple-element.51.queries, bf16[256,128]{1,0:T(8,128)(2,1)} %get-tuple-element.52.keys, bf16[256,128]{1,0:T(8,128)(2,1)} %get-tuple-element.53.values, ...), custom_call_target="tpu_custom_call" | custom-call | flops 3221225472 | bytes 16777216 | tf_op jit(solution)/shard_map/pallas_call | solution.py:1039
  132.2 55.7 %shard_map.143 = (f32[32,4096]{1,0:T(8,128)}, bf16[8,32,4096]{2,1,0:T(8,128)(2,1)}, f32[256,768]{1,0:T(8,128)}, bf16[4,256,512]{2,1,0:T(8,128)(2,1)}) custom-call(bf16[8,32,4096]{2,1,0:T(8,128)(2,1)} %bitcast.27, bf16[4,8,32,1024]{3,2,1,0:T(8,128)(2,1)} %bitcast.28, bf16[32,4096]{1,0:T(8,128)(2,1)} %get-tuple-element.58.stream_in, ...), custom_call_target="tpu_custom_call" | custom-call | tf_op jit(solution)/shard_map/pallas_call | solution.py:567
  187.9 14.8 %shard_map.144 = (bf16[256,4096]{1,0:T(8,128)(2,1)}, bf16[1024,1024]{1,0:T(8,128)(2,1)}) custom-call(s32[1]{0:T(128)} %dynamic_slice.5.lengths, bf16[256,512]{1,0:T(8,128)(2,1)} %get-tuple-element.48.queries, bf16[256,128]{1,0:T(8,128)(2,1)} %get-tuple-element.49.keys, bf16[256,128]{1,0:T(8,128)(2,1)} %get-tuple-element.50.values, ...), custom_call_target="tpu_custom_call" | custom-call | flops 3221225472 | bytes 16777216 | tf_op jit(solution)/shard_map/pallas_call | solution.py:1039
  202.7 47.7 %shard_map.145 = (f32[32,4096]{1,0:T(8,128)}, bf16[8,32,4096]{2,1,0:T(8,128)(2,1)}, bf16[4,32,1024]{2,1,0:T(8,128)(2,1)}) custom-call(bf16[8,32,4096]{2,1,0:T(8,128)(2,1)} %bitcast.31, bf16[4,8,32,1024]{3,2,1,0:T(8,128)(2,1)} %bitcast.32, f32[32,4096]{1,0:T(8,128)} %get-tuple-element.66.tangent, f32[32,1]{1,0:T(8,128)} %fusion.5.mask), custom_call_target="tpu_custom_call" | custom-call | tf_op jit(solution)/shard_map/pallas_call | solution.py:567
  250.3 13.5 %shard_map.146 = (bf16[256,768]{1,0:T(8,128)(2,1)}, bf16[256,4096]{1,0:T(8,128)(2,1)}) custom-call(s32[1]{0:T(128)} %dynamic_slice.5.lengths, bf16[256,4096]{1,0:T(8,128)(2,1)} %bitcast.25, bf16[2,512,4096]{2,1,0:T(8,128)(2,1)} %out_weight.7, bf16[256,512]{1,0:T(8,128)(2,1)} %get-tuple-element.48.queries, bf16[256,128]{1,0:T(8,128)(2,1)} %get-tuple-element.49.keys, ...), custom_call_target="tpu_custom_call" | custom-call | flops 3221225472 | bytes 16777216 | tf_op jit(solution)/shard_map/pallas_call | solution.py:1091
  263.8 50.3 %shard_map.147 = (bf16[8,32,4096]{2,1,0:T(8,128)(2,1)}, bf16[4,8,32,1024]{3,2,1,0:T(8,128)(2,1)}, bf16[4,256,768]{2,1,0:T(8,128)(2,1)}, bf16[4,32,1024]{2,1,0:T(8,128)(2,1)}) custom-call(bf16[8,32,4096]{2,1,0:T(8,128)(2,1)} %bitcast.29, bf16[32,4096]{1,0:T(8,128)(2,1)} %get-tuple-element.58.stream_in, f32[1,4096]{1,0:T(1,128)} %get-tuple-element.78.gain, ...), custom_call_target="tpu_custom_call" | custom-call | tf_op jit(solution)/shard_map/pallas_call | solution.py:567
  314.2 8.0 %shard_map.148.grads = bf16[256,768]{1,0:T(8,128)(2,1)} custom-call(s32[1]{0:T(128)} %dynamic_slice.5.lengths, bf16[256,4096]{1,0:T(8,128)(2,1)} %bitcast.43, bf16[2,512,4096]{2,1,0:T(8,128)(2,1)} %out_weight.7, bf16[256,512]{1,0:T(8,128)(2,1)} %get-tuple-element.51.queries, bf16[256,128]{1,0:T(8,128)(2,1)} %get-tuple-element.52.keys, ...), custom_call_target="tpu_custom_call" | custom-call | flops 3221225472 | bytes 16777216 | tf_op jit(solution)/shard_map/pallas_call | solution.py:1091
  322.1 40.4 %shard_map.149 = (bf16[4,256,768]{2,1,0:T(8,128)(2,1)}, bf16[4,8,32,1024]{3,2,1,0:T(8,128)(2,1)}) custom-call(bf16[256,768]{1,0:T(8,128)(2,1)} %shard_map.148.grads, bf16[4,32,1024]{2,1,0:T(8,128)(2,1)} %get-tuple-element.73.pieces_in), custom_call_target="tpu_custom_call" | custom-call | tf_op jit(solution)/shard_map/pallas_call | solution.py:567
  362.5 14.2 %shard_map.150 = (f32[2,1024,512]{2,1,0:T(8,128)}, f32[2,1024,128]{2,1,0:T(8,128)}, f32[2,1024,128]{2,1,0:T(8,128)}, f32[2,512,1024]{2,1,0:T(8,128)}) custom-call(bf16[1024,1024]{1,0:T(8,128)(2,1)} %bitcast.34, bf16[1024,768]{1,0:T(8,128)(2,1)} %bitcast.46, bf16[1024,512]{1,0:T(8,128)(2,1)} %bitcast.39, bf16[1024,1024]{1,0:T(8,128)(2,1)} %bitcast.44, ...), custom_call_target="tpu_custom_call" | custom-call | flops 4294967296 | bytes 33554432 | tf_op jit(solution)/shard_map/pallas_call | solution.py:1134
  (2 shorter events, 0.0 us)
